TPU v7x, 32 devices: a whole 2x2x4 slice. The times are simulated.
32 devices in a mesh: gz: 2 (over x), gx: 4 (over y, core), gy: 4 (over z).
Axes of the slice: x: 2, y: 2, z: 4, core: 2. Of those that a mesh axis runs over, the one named last changes fastest.
Arguments:
- right_side: float32 [16, 3, 32, 1024], P('gz', None, 'gy', 'gx'), may hold values from -6 to 6
- start_field: float32 [16, 3, 32, 1024], P('gz', None, 'gy', 'gx'), may hold values from -6 to 6
- layer_material: int32 [16], P('gz'), may hold values from 0 to 7
- stiffness: float32 [8, 3, 3, 3], replicated, may hold values from -0.2 to 8, as said below
- line_factors: float32 [8, 3, 3, 3], replicated, may hold values from -0.05 to 1
Outputs:
- solution_field: float32 [16, 3, 32, 1024], P('gz', None, 'gy', 'gx')
- final_residual: float32 [16, 3, 32, 1024], P('gz', None, 'gy', 'gx')
Inputs may be any that keep to these rules, and one draw needn't show every extreme that they name: `stiffness`: diagonal blocks dominate each row over the lateral and vertical couplings of the stencil.
All inputs are finite; a program needn't handle non-finite values.
Results may differ from a plain program's by a relative error of at most 0.0001.
Values sent between devices are 32-bit elements; how exact they have to be, the bound alone decides.
A program may use at most 64 MiB of HBM per device.

v0:
```python
import jax
import jax.numpy as jnp
from jax import lax
from jax.sharding import PartitionSpec as P

SWEEPS = 3


def with_halo(cells, sides, width):
    for axis, dim in sides:
        count = lax.axis_size(axis)
        ends = count - 1
        head = lax.slice_in_dim(cells, 0, width, axis=dim)
        tail = lax.slice_in_dim(cells, cells.shape[dim] - width, cells.shape[dim], axis=dim)
        cells = jnp.concatenate(
            [
                lax.ppermute(tail, axis, [(i, (i + 1) % count) for i in range(ends)]),
                cells,
                lax.ppermute(head, axis, [((i + 1) % count, i) for i in range(ends)]),
            ],
            axis=dim,
        )
    return cells


def prefix(value, axis, join, neutral, backward):
    count, mine = (lax.axis_size(axis), lax.axis_index(axis))
    pieces = jax.tree.map(lambda part: lax.all_gather(part, axis), value)
    if backward:
        pieces = jax.tree.map(lambda part: part[::-1], pieces)
        mine = count - 1 - mine
    subtotal = jax.tree.map(
        lambda part, zero: jnp.full_like(part, 0) + jnp.asarray(zero, part.dtype), value, neutral
    )

    def lap(position, subtotal):
        longer = join(subtotal, jax.tree.map(lambda part: part[position], pieces))
        return jax.tree.map(lambda new, old: jnp.where(position < mine, new, old), longer, subtotal)

    return lax.fori_loop(0, count - 1, lap, subtotal)


def apply_block(blocks, field):
    columns = []
    for row_index in range(3):
        summed = blocks[..., row_index, 0, None, None] * field[..., 0, :, :]
        for col_index in (1, 2):
            summed = (
                summed + blocks[..., row_index, col_index, None, None] * field[..., col_index, :, :]
            )
        columns.append(summed)
    return jnp.stack(columns, axis=-3)


def chain_link(earlier, later):
    earlier_map, earlier_vec = earlier
    later_map, later_vec = later
    joined = jnp.matmul(later_map, earlier_map, precision=lax.Precision.HIGHEST)
    return (joined, later_vec + apply_block(later_map, earlier_vec))


def running_chain(multipliers, sources):

    def advance(carry, item):
        joined = chain_link(carry, item)
        return (joined, joined)

    start = (jnp.eye(3, dtype=jnp.float32), jnp.zeros(sources.shape[1:], jnp.float32))
    _, (maps, vectors) = lax.scan(advance, start, (multipliers, sources), unroll=True)
    return (maps, vectors)


def layer_blocks(table, layer_ids):
    onehot = (layer_ids[:, None] == jnp.arange(table.shape[0])[None, :]).astype(jnp.float32)
    return jnp.sum(onehot[:, :, None, None, None] * table[None], axis=1)


def padded_field(field):
    return with_halo(field, (("gz", 0), ("gx", 3), ("gy", 2)), 1)


def operate(field, diag_block, lateral_block, vertical_block):
    padded = padded_field(field)
    lateral = padded[1:-1, :, 1:-1, 2:] + padded[1:-1, :, 1:-1, :-2]
    lateral = lateral + padded[1:-1, :, 2:, 1:-1] + padded[1:-1, :, :-2, 1:-1]
    vertical = padded[2:, :, 1:-1, 1:-1] + padded[:-2, :, 1:-1, 1:-1]
    return (
        apply_block(diag_block, field)
        - apply_block(lateral_block, lateral)
        - apply_block(vertical_block, vertical)
    )


def line_solve(resid, factor_blocks):
    identity = (jnp.eye(3, dtype=jnp.float32), jnp.zeros(resid.shape[1:], jnp.float32))
    weighted = apply_block(factor_blocks[:, 0], resid)
    forward_maps, upward = running_chain(factor_blocks[:, 1], weighted)
    forward_in = prefix((forward_maps[-1], upward[-1]), "gz", chain_link, identity, False)
    upward = upward + apply_block(forward_maps, forward_in[1][None])
    backward_maps, downward = running_chain(factor_blocks[::-1, 2], upward[::-1])
    backward_in = prefix((backward_maps[-1], downward[-1]), "gz", chain_link, identity, True)
    downward = downward + apply_block(backward_maps, backward_in[1][None])
    return downward[::-1]


def on_device(right_side, start_field, layer_material, stiffness, line_factors):
    load, field = (right_side, start_field)
    fine_sten = layer_blocks(stiffness, layer_material)
    coarse_sten = layer_blocks(stiffness, layer_material[0::2])
    fine_fac = layer_blocks(line_factors, layer_material)
    coarse_fac = layer_blocks(line_factors, layer_material[0::2])
    fine_args = (fine_sten[:, 0], fine_sten[:, 1], fine_sten[:, 2])
    coarse_args = (coarse_sten[:, 0], coarse_sten[:, 1], 0.25 * coarse_sten[:, 2])
    for counter in range(SWEEPS):
        field = field + line_solve(load - operate(field, *fine_args), fine_fac)
    resid = load - operate(field, *fine_args)
    paired = resid.reshape(resid.shape[0] // 2, 2, 3, resid.shape[2], resid.shape[3])
    coarse_rhs = paired[:, 0] + paired[:, 1]
    correction = line_solve(coarse_rhs, coarse_fac)
    for counter in range(SWEEPS - 1):
        correction = correction + line_solve(
            coarse_rhs - operate(correction, *coarse_args), coarse_fac
        )
    solution_field = field + jnp.repeat(correction, 2, axis=0)
    final_residual = load - operate(solution_field, *fine_args)
    return (solution_field, final_residual)


def solution(mesh):
    return jax.shard_map(
        on_device,
        mesh=mesh,
        in_specs=(P("gz", None, "gy", "gx"), P("gz", None, "gy", "gx"), P("gz"), P(), P()),
        out_specs=(P("gz", None, "gy", "gx"), P("gz", None, "gy", "gx")),
        check_vma=False,
    )
```

profile of v0, /device:TPU:28, one launch (start us, length us, event | category | flops | bytes accessed | tf_op | source)
XLA Modules:
  0.0 655.3 jit_solution(6568165284293828513)
XLA Ops:
  107.8 5.6 multiply_add_fusion.260
  113.4 5.6 multiply_add_fusion.257
  119.0 5.6 multiply_add_fusion.254
  130.3 5.7 multiply_add_fusion.248
  136.1 5.7 multiply_add_fusion.245
  157.9 5.7 multiply_add_fusion.239
  169.1 5.7 multiply_add_fusion.233
  186.1 5.7 add_bitcast_fusion.32
  224.0 5.6 multiply_add_fusion.224
  229.6 5.6 multiply_add_fusion.221
  235.3 5.6 multiply_add_fusion.218
  246.5 5.7 multiply_add_fusion.212
  252.3 5.7 multiply_add_fusion.209
  274.1 5.7 multiply_add_fusion.203
  285.4 5.7 multiply_add_fusion.197
  302.2 5.7 add_bitcast_fusion.26
  343.8 5.6 multiply_add_fusion.185
  349.5 5.6 multiply_add_fusion.182
  360.7 5.7 multiply_add_fusion.176
  366.5 5.7 multiply_add_fusion.173
  388.3 5.7 multiply_add_fusion.167
  399.6 5.7 multiply_add_fusion.161
  416.4 5.7 add_bitcast_fusion.20
  462.9 5.7 add_bitcast_fusion.17
  473.5 5.7 multiply_add_fusion.146
  484.6 5.9 add_bitcast_fusion.14
  530.1 5.7 add_bitcast_fusion.11
  540.7 5.7 multiply_add_fusion.134
  551.8 5.9 add_bitcast_fusion.8
  597.4 5.7 add_bitcast_fusion.5
  608.0 5.7 multiply_add_fusion.122
  619.1 5.9 add_bitcast_fusion.2
  (492 shorter events, 425.5 us)
Async XLA Ops:
  1.4 87.8 %collective-permute-start = (f32[1,3,8,256]{3,2,1,0:T(8,128)S(1)}, f32[1,3,8,256]{3,2,1,0:T(8,128)S(1)}, u32[]{:S(2)}, u32[]{:S(2)}) collective-permute-start(f32[1,3,8,256]{3,2,1,0:T(8,128)S(1)} %get-tuple-element.398), channel_id=1, source_target_pairs={{0,16},{1,17},{2,18},{3,19},{4,20},{5,21},{6,22},{7,23},{8,24},{9,... | collective-permute-start | bytes 73736 | tf_op jit(solution)/shard_map/ppermute | solution.py:17
  4.9 84.2 %collective-permute-start.1 = (f32[1,3,8,256]{3,2,1,0:T(8,128)S(1)}, f32[1,3,8,256]{3,2,1,0:T(8,128)S(1)}, u32[]{:S(2)}, u32[]{:S(2)}) collective-permute-start(f32[1,3,8,256]{3,2,1,0:T(8,128)S(1)} %get-tuple-element.397), channel_id=1, source_target_pairs={{16,0},{17,1},{18,2},{19,3},{20,4},{21,5},{22,6},{23,7},{24,8},{25... | collective-permute-start | bytes 73736 | tf_op jit(solution)/shard_map/ppermute | solution.py:19
  89.3 4.4 collective-permute-start.2
  91.3 6.2 collective-permute-start.3
  100.2 6.0 collective-permute-start.5
  196.6 5.5 collective-permute-start.6
  200.5 5.7 collective-permute-start.7
  206.4 4.4 collective-permute-start.8
  208.3 6.2 collective-permute-start.9
  214.8 4.1 collective-permute-start.10
  217.2 6.0 collective-permute-start.11
  314.7 5.7 collective-permute-start.13
  320.6 4.4 collective-permute-start.14
  322.5 6.2 collective-permute-start.15
  329.0 4.1 collective-permute-start.16
  331.4 6.0 collective-permute-start.17
  428.9 5.7 collective-permute-start.19
  434.7 4.4 collective-permute-start.20
  436.7 6.2 collective-permute-start.21
  445.1 6.0 collective-permute-start.23
  497.2 5.7 collective-permute-start.25
  503.0 4.4 collective-permute-start.26
  504.9 5.7 collective-permute-start.27
  512.8 5.8 collective-permute-start.29
  564.4 5.7 collective-permute-start.31
  570.2 4.4 collective-permute-start.32
  572.2 5.7 collective-permute-start.33
  580.1 5.8 collective-permute-start.35
  631.8 5.7 collective-permute-start.37
  637.6 4.4 collective-permute-start.38
  639.5 6.2 collective-permute-start.39
  648.1 6.0 collective-permute-start.41
  (16 other events, 91.2 us)
where the time goes:
time: 662 us; the launch traced here: 655 us
  other arithmetic  352 us (53%)
  waiting for transfers between devices  81.8 us (12%)
  starting transfers between devices  80.4 us (12%)
  blocking collectives  71.9 us (11%)
  between operations  47.7 us (7%)
  local copies, waits for them, and re-layouts  18.2 us (3%)
    add x87, other arithmetic, apply_block(): summed + blocks[..., row_index, col_index, None, None] * field[..., col_i...  274 us
    all_gather x16, blocking collectives, prefix(): pieces = jax.tree.map(lambda part: lax.all_gather(part, axis), value)  71.9 us
    another operation x26, other arithmetic, apply_block(): return jnp.stack(columns, axis=-3)  68.8 us
    ppermute x21, waiting for transfers between devices, with_halo(): lax.ppermute(tail, axis, [(i, (i + 1) % count) for i in range(ends)])  55.2 us
    ppermute x21, starting transfers between devices, with_halo(): lax.ppermute(tail, axis, [(i, (i + 1) % count) for i in range(ends)])  43 us
    ppermute x21, starting transfers between devices, with_halo(): lax.ppermute(head, axis, [((i + 1) % count, i) for i in range(ends)])  37.4 us
    ppermute x21, waiting for transfers between devices, with_halo(): lax.ppermute(head, axis, [((i + 1) % count, i) for i in range(ends)])  26.6 us
  transfers between devices with their start and end apart: 42, of which 29 were waited for; matrix products, arithmetic and copies ran while one was open for 3% of the time, Pallas kernels for 0%

commit v1 on v0

v1 whole, which is shorter than its diff:
```python
import functools

import jax
import jax.numpy as jnp
from jax import lax
from jax.experimental import pallas as pl
from jax.experimental.pallas import tpu as pltpu
from jax.sharding import PartitionSpec as P

SWEEPS = 3
MESH = pl.DeviceIdType.MESH


def total(terms):
    result = terms[0]
    for term in terms[1:]:
        result = result + term
    return result


def kernel(
    sizes, material, sten, fac, load, start, out_u, out_r,
    cor, crhs, res, loc, chain, below, above, cbelow, cabove,
    row_out, row_in, crow_out, crow_in, col_out, col_in,
    gather, maps,
    row_ss, row_rs, col_ss, col_rs, z_ss, z_rs, map_ss, map_rs, zh_ss, zh_rs,
):
    nz, ny, nx = sizes
    layers, comps, rows, lanes = load.shape
    half = layers // 2
    gz, gy, gx = (lax.axis_index(name) for name in ("gz", "gy", "gx"))
    wide = col_in.shape[-1]
    row_id = lax.broadcasted_iota(jnp.int32, (rows, lanes), 0)
    lane_id = lax.broadcasted_iota(jnp.int32, (rows, lanes), 1)
    col_id = lax.broadcasted_iota(jnp.int32, (rows, wide), 1)
    top, bottom = row_id == 0, row_id == rows - 1
    first, last = lane_id == 0, lane_id == lanes - 1
    three = range(comps)
    pending = []

    def block(table, level, layer, which):
        base = material[layer * (2 if level else 1)] * 27 + which * 9
        scale = 0.25 if level and table is sten and which == 2 else None
        values = [[table[base + i * 3 + j] for j in three] for i in three]
        if scale is not None:
            values = [[scale * v for v in line] for line in values]
        return values

    def times(mat, vec):
        return [total([mat[i][j] * vec[j] for j in three]) for i in three]

    def at(z, y, x):
        return {"gz": z, "gy": y, "gx": x}

    def copy_if(cond, src, dst, ss, rs, target):
        copy = pltpu.make_async_remote_copy(
            src_ref=src, dst_ref=dst, send_sem=ss, recv_sem=rs,
            device_id=target, device_id_type=MESH,
        )

        @pl.when(cond)
        def _():
            copy.start()

        pending.append((cond, copy))

    def arrive_if(cond, ref, ss, rs):
        @pl.when(cond)
        def _():
            pltpu.make_async_remote_copy(
                src_ref=ref, dst_ref=ref, send_sem=ss, recv_sem=rs,
                device_id=at(gz, gy, gx), device_id_type=MESH,
            ).wait_recv()

    has_prev_y, has_next_y = gy > 0, gy < ny - 1
    has_prev_x, has_next_x = gx > 0, gx < nx - 1
    has_below, has_above = gz > 0, gz < nz - 1

    barrier = pltpu.get_barrier_semaphore()
    peers = [(gz != j, at(j, gy, gx)) for j in range(nz)]
    peers += [(has_prev_y, at(gz, gy - 1, gx)), (has_next_y, at(gz, gy + 1, gx))]
    peers += [(has_prev_x, at(gz, gy, gx - 1)), (has_next_x, at(gz, gy, gx + 1))]
    for cond, target in peers:
        @pl.when(cond)
        def _(target=target):
            pl.semaphore_signal(barrier, inc=1, device_id=target, device_id_type=MESH)

    for side, cond in enumerate((has_prev_y, has_next_y)):
        @pl.when(jnp.logical_not(cond))
        def _(side=side):
            row_in[:, side] = jnp.zeros_like(row_in[:, side])
            crow_in[:, side] = jnp.zeros_like(crow_in[:, side])
    for side, cond in enumerate((has_prev_x, has_next_x)):
        @pl.when(jnp.logical_not(cond))
        def _(side=side):
            col_in[:, side] = jnp.zeros_like(col_in[:, side])
    for cond, ref in ((has_below, below), (has_above, above)):
        @pl.when(jnp.logical_not(cond))
        def _(ref=ref):
            ref[...] = jnp.zeros_like(ref)
    for j in range(nz):
        @pl.when(gz > j)
        def _(j=j):
            gather[:, 1, j] = jnp.zeros_like(gather[:, 1, j])

    basis_lane = lax.broadcasted_iota(jnp.int32, (8, 128), 1)
    basis = [(basis_lane == c).astype(jnp.float32) for c in three]
    for level, count in ((0, layers), (1, half)):
        ups = []
        carry = basis
        for layer in range(count):
            carry = times(block(fac, level, layer, 1), carry)
            ups.append(carry)
        turned, back = None, basis
        for layer in reversed(range(count)):
            mat = block(fac, level, layer, 2)
            turned = ups[layer] if turned is None else [
                a + b for a, b in zip(ups[layer], times(mat, turned))
            ]
            back = times(mat, back)
            if layer == count - 1:
                edge = back
        for kind, value in enumerate((ups[-1], turned, back, edge)):
            for c in three:
                maps[gz, level, kind, c] = value[c]

    def held(level, owner, kind):
        tiles = [maps[owner, level, kind, c] for c in three]
        return [[jnp.broadcast_to(tiles[i][:rows, j : j + 1], (rows, lanes)) for j in three] for i in three]

    def send_sides(phase, level, field, count):
        out, into = (crow_out, crow_in) if level else (row_out, row_in)
        slot = phase - SWEEPS - 1 if level else (phase if phase <= SWEEPS else SWEEPS + 1)
        tiles = [jnp.zeros((rows, wide), jnp.float32)] * 2
        for layer in range(count):
            for c in three:
                spot = layer * comps + c
                value = field[layer, c]
                out[slot, 0, spot : spot + 1, :] = value[rows - 1 : rows, :]
                out[slot, 1, spot : spot + 1, :] = value[0:1, :]
                here = col_id == spot
                tiles[0] = jnp.where(here, value[:, lanes - 1 : lanes], tiles[0])
                tiles[1] = jnp.where(here, value[:, 0:1], tiles[1])
        for side in range(2):
            col_out[phase, side] = tiles[side]
        for side, cond, target in (
            (0, has_next_y, at(gz, gy + 1, gx)), (1, has_prev_y, at(gz, gy - 1, gx)),
        ):
            copy_if(cond, out.at[slot, side], into.at[slot, side],
                    row_ss.at[phase, side], row_rs.at[phase, side], target)
        for side, cond, target in (
            (0, has_next_x, at(gz, gy, gx + 1)), (1, has_prev_x, at(gz, gy, gx - 1)),
        ):
            copy_if(cond, col_out.at[phase, side], col_in.at[phase, side],
                    col_ss.at[phase, side], col_rs.at[phase, side], target)
        return phase, slot, into

    def await_sides(handle):
        phase, slot, into = handle
        for side, cond in enumerate((has_prev_y, has_next_y)):
            arrive_if(cond, into.at[slot, side], row_ss.at[phase, side], row_rs.at[phase, side])
        for side, cond in enumerate((has_prev_x, has_next_x)):
            arrive_if(cond, col_in.at[phase, side], col_ss.at[phase, side], col_rs.at[phase, side])

    def inner_residual(level, field, source, low, high, count):
        for layer in range(count):
            here = [field[layer, c] for c in three]
            side, vert = [], []
            for c in three:
                x = here[c]
                side.append(
                    (jnp.where(first, 0.0, pltpu.roll(x, 1, 1)) + jnp.where(last, 0.0, pltpu.roll(x, lanes - 1, 1)))
                    + (jnp.where(top, 0.0, pltpu.roll(x, 1, 0)) + jnp.where(bottom, 0.0, pltpu.roll(x, rows - 1, 0)))
                )
                under = field[layer - 1, c] if layer else low[c]
                over = field[layer + 1, c] if layer < count - 1 else high[c]
                vert.append(under + over)
            a = times(block(sten, level, layer, 0), here)
            b = times(block(sten, level, layer, 1), side)
            d = times(block(sten, level, layer, 2), vert)
            for c in three:
                res[layer, c] = source[layer, c] - (a[c] - b[c] - d[c])

    def full_residual(level, handle, layer):
        phase, slot, into = handle
        edge = []
        for c in three:
            spot = layer * comps + c
            line = jnp.where(top, into[slot, 0, spot : spot + 1, :], 0.0)
            line = jnp.where(bottom, into[slot, 1, spot : spot + 1, :], line)
            post = jnp.where(first, col_in[phase, 0][:, spot : spot + 1], 0.0)
            post = jnp.where(last, col_in[phase, 1][:, spot : spot + 1], post)
            edge.append(line + post)
        extra = times(block(sten, level, layer, 1), edge)
        return [res[layer, c] + extra[c] for c in three]

    def line_solve(level, turn, resid, count):
        carry = None
        for layer in range(count):
            now = times(block(fac, level, layer, 0), resid(layer))
            if carry is not None:
                now = [a + b for a, b in zip(now, times(block(fac, level, layer, 1), carry))]
            for c in three:
                chain[layer, c] = now[c]
            carry = now
        for c in three:
            gather[turn, 0, gz, c] = carry[c]
        if nz > 1:
            for j in range(nz):
                copy_if(jnp.logical_and(gz != j, gz < nz - 1), gather.at[turn, 0, gz], gather.at[turn, 0, gz],
                        z_ss.at[turn, 0, j], z_rs.at[turn, 0, gz], at(j, gy, gx))
        back = None
        for layer in reversed(range(count)):
            now = [chain[layer, c] for c in three]
            if back is not None:
                now = [a + b for a, b in zip(now, times(block(fac, level, layer, 2), back))]
            for c in three:
                loc[layer, c] = now[c]
            back = now
        for c in three:
            gather[turn, 1, gz, c] = back[c]
        for j in range(nz):
            copy_if(gz > j, gather.at[turn, 1, gz], gather.at[turn, 1, gz],
                    z_ss.at[turn, 1, j], z_rs.at[turn, 1, gz], at(j, gy, gx))
        for j in range(nz - 1):
            arrive_if(gz != j, gather.at[turn, 0, j], z_ss.at[turn, 0, j], z_rs.at[turn, 0, j])
        for j in range(1, nz):
            arrive_if(gz < j, gather.at[turn, 1, j], z_ss.at[turn, 1, j], z_rs.at[turn, 1, j])
        zero = [jnp.zeros((rows, lanes), jnp.float32)] * 3
        ins, outs = [zero], [zero]
        for k in range(nz - 1):
            value = [gather[turn, 0, k, c] for c in three]
            if k:
                value = [a + b for a, b in zip(value, times(held(level, k, 0), ins[k]))]
            ins.append(value)
        for k in reversed(range(1, nz)):
            value = [gather[turn, 1, k, c] + b for c, b in enumerate(times(held(level, k, 1), ins[k]))]
            if k < nz - 1:
                value = [a + b for a, b in zip(value, times(held(level, k, 2), outs[0]))]
            outs.insert(0, value)
        enter, leave = ins[0], outs[0]
        for k in range(1, nz):
            enter = [jnp.where(gz == k, a, b) for a, b in zip(ins[k], enter)]
            leave = [jnp.where(gz == k, a, b) for a, b in zip(outs[k], leave)]
        carry = enter
        for layer in range(count):
            carry = times(block(fac, level, layer, 1), carry)
            for c in three:
                chain[layer, c] = carry[c]
        carry = leave
        for layer in reversed(range(count)):
            carry = [chain[layer, c] + b for c, b in enumerate(times(block(fac, level, layer, 2), carry))]
            for c in three:
                loc[layer, c] = loc[layer, c] + carry[c]
        under = times(held(level, jnp.maximum(gz - 1, 0), 3), [loc[0, c] for c in three])
        under = [jnp.where(has_below, enter[c] + under[c], 0.0) for c in three]
        return under, leave

    pl.semaphore_wait(barrier, total([cond.astype(jnp.int32) for cond, _ in peers]))

    handle = send_sides(0, 0, start, layers)
    copy_if(has_above, start.at[layers - 1], below, zh_ss.at[0], zh_rs.at[0], at(gz + 1, gy, gx))
    copy_if(has_below, start.at[0], above, zh_ss.at[1], zh_rs.at[1], at(gz - 1, gy, gx))
    for j in range(nz):
        copy_if(gz != j, maps.at[gz], maps.at[gz], map_ss.at[j], map_rs.at[gz], at(j, gy, gx))
    arrive_if(has_below, below, zh_ss.at[0], zh_rs.at[0])
    arrive_if(has_above, above, zh_ss.at[1], zh_rs.at[1])
    for sweep in range(SWEEPS + 1):
        field = out_u if sweep else start
        inner_residual(0, field, load, below, above, layers)
        await_sides(handle)
        if sweep == SWEEPS:
            break
        if sweep == 0:
            for j in range(nz):
                arrive_if(gz != j, maps.at[j], map_ss.at[j], map_rs.at[j])
        under, over = line_solve(0, sweep, functools.partial(full_residual, 0, handle), layers)
        for layer in range(layers):
            for c in three:
                out_u[layer, c] = field[layer, c] + loc[layer, c]
        for c in three:
            below[c] = below[c] + under[c]
            above[c] = above[c] + over[c]
        handle = send_sides(sweep + 1, 0, out_u, layers)

    for k in range(half):
        pair = [full_residual(0, handle, 2 * k + step) for step in range(2)]
        for c in three:
            crhs[k, c] = pair[0][c] + pair[1][c]
    for sweep in range(SWEEPS):
        if sweep:
            inner_residual(1, cor, crhs, cbelow, cabove, half)
            await_sides(handle)
            source = functools.partial(full_residual, 1, handle)
        else:
            def source(layer):
                return [crhs[layer, c] for c in three]
        under, over = line_solve(1, SWEEPS + sweep, source, half)
        for layer in range(half):
            for c in three:
                value = loc[layer, c]
                cor[layer, c] = cor[layer, c] + value if sweep else value
        for c in three:
            cbelow[c] = cbelow[c] + under[c] if sweep else under[c]
            cabove[c] = cabove[c] + over[c] if sweep else over[c]
        if sweep < SWEEPS - 1:
            handle = send_sides(SWEEPS + 1 + sweep, 1, cor, half)
    for layer in range(layers):
        for c in three:
            out_u[layer, c] = out_u[layer, c] + cor[layer // 2, c]
    for c in three:
        below[c] = below[c] + cbelow[c]
        above[c] = above[c] + cabove[c]
    handle = send_sides(2 * SWEEPS, 0, out_u, layers)
    inner_residual(0, out_u, load, below, above, layers)
    await_sides(handle)
    for layer in range(layers):
        value = full_residual(0, handle, layer)
        for c in three:
            out_r[layer, c] = value[c]
    for cond, copy in pending:
        @pl.when(cond)
        def _(copy=copy):
            copy.wait_send()


def solution(mesh):
    sizes = tuple(mesh.shape[name] for name in ("gz", "gy", "gx"))
    nz = sizes[0]

    def on_device(right_side, start_field, layer_material, stiffness, line_factors):
        layers, comps, rows, lanes = right_side.shape
        half = layers // 2
        wide = -(-layers * comps // 128) * 128
        phases = 2 * SWEEPS + 1
        f32 = jnp.float32
        vmem = pl.BlockSpec(memory_space=pltpu.VMEM)
        smem = pl.BlockSpec(memory_space=pltpu.SMEM)
        dma = pltpu.SemaphoreType.DMA
        scratch = [
            pltpu.VMEM((half, comps, rows, lanes), f32),
            pltpu.VMEM((half, comps, rows, lanes), f32),
            pltpu.VMEM((layers, comps, rows, lanes), f32),
            pltpu.VMEM((layers, comps, rows, lanes), f32),
            pltpu.VMEM((layers, comps, rows, lanes), f32),
        ]
        scratch += [pltpu.VMEM((comps, rows, lanes), f32)] * 4
        scratch += [pltpu.VMEM((SWEEPS + 2, 2, layers * comps, lanes), f32)] * 2
        scratch += [pltpu.VMEM((SWEEPS - 1, 2, half * comps, lanes), f32)] * 2
        scratch += [pltpu.VMEM((phases, 2, rows, wide), f32)] * 2
        scratch += [
            pltpu.VMEM((2 * SWEEPS, 2, nz, comps, rows, lanes), f32),
            pltpu.VMEM((nz, 2, 4, comps, 8, 128), f32),
        ]
        scratch += [dma((phases, 2))] * 4 + [dma((2 * SWEEPS, 2, nz))] * 2
        scratch += [dma((nz,))] * 2 + [dma((2,))] * 2
        out = jax.ShapeDtypeStruct(right_side.shape, f32)
        return pl.pallas_call(
            functools.partial(kernel, sizes),
            out_shape=(out, out),
            in_specs=[smem, smem, smem, vmem, vmem],
            out_specs=(vmem, vmem),
            scratch_shapes=scratch,
            compiler_params=pltpu.CompilerParams(collective_id=0, has_side_effects=True),
        )(layer_material, stiffness.reshape(-1), line_factors.reshape(-1), right_side, start_field)

    return jax.shard_map(
        on_device,
        mesh=mesh,
        in_specs=(P("gz", None, "gy", "gx"), P("gz", None, "gy", "gx"), P("gz"), P(), P()),
        out_specs=(P("gz", None, "gy", "gx"), P("gz", None, "gy", "gx")),
        check_vma=False,
    )
```

time: 662 us -> 54.8 us (0.08)
  the two profiles are of different devices: /device:TPU:28 before, /device:TPU:0 now
where the time goes in v1:
time: 54.8 us; the launch traced here: 54.6 us
  Pallas kernels  49.2 us (90%)
  local copies, waits for them, and re-layouts  4.76 us (9%)
  between operations  0.65 us (1%)
    pallas_call x1, Pallas kernels, on_device(): pl.pallas_call(functools.partial(kernel, sizes), out_shape=(out, out), in...  49.2 us
    unnamed x8, local copies, waits for them, and re-layouts  3.33 us

profile of v1, /device:TPU:0, one launch (start us, length us, event | category | flops | bytes accessed | tf_op | source)
XLA Modules:
  0.0 54.6 jit_solution(11455159818172251733)
XLA Ops:
  0.6 0.9 %copy.7 = f32[8,3,3,3]{3,2,1,0:T(4,128)S(1)} copy(f32[8,3,3,3]{0,3,2,1:T(4,128)} %param.8) | data formatting | bytes 1728 | tf_op args[3]
  1.5 0.0 copy-start.1
  1.5 0.7 %reshape.10.sten = f32[216]{0:T(256)} reshape(f32[8,3,3,3]{3,2,1,0:T(4,128)S(1)} %copy.7) | data formatting | bytes 1728 | tf_op jit(solution)/shard_map/reshape | solution.py:365
  2.2 0.0 copy-done.1
  2.2 0.1 copy.8
  2.3 0.7 %reshape.11.fac = f32[216]{0:T(256)} reshape(f32[8,3,3,3]{3,2,1,0:T(4,128)S(1)} %copy.8) | data formatting | bytes 1728 | tf_op jit(solution)/shard_map/reshape | solution.py:365
  3.1 49.2 %shard_map.68 = (f32[8,3,8,256]{3,2,1,0:T(8,128)}, f32[8,3,8,256]{3,2,1,0:T(8,128)}) custom-call(s32[8]{0:T(128)} %material.1, f32[216]{0:T(256)} %reshape.10.sten, f32[216]{0:T(256)} %reshape.11.fac, f32[8,3,8,256]{3,2,1,0:T(8,128)} %load.1, f32[8,3,8,256]{3,2,1,0:T(8,128)} %start.1), custom_call_target="tpu_custom_call" | custom-call | tf_op jit(solution)/shard_map/pallas_call | solution.py:358
  52.2 0.0 copy-start
  52.2 1.7 %copy.11 = f32[8,3,8,256]{3,2,1,0:T(8,128)} copy(f32[8,3,8,256]{3,2,1,0:T(8,128)} %get-tuple-element.4) | data formatting | bytes 393216
  53.9 0.0 copy-done
  53.9 0.7 %copy.12 = f32[8,3,8,256]{3,2,1,0:T(8,128)} copy(f32[8,3,8,256]{3,2,1,0:T(8,128)S(1)} %copy-done) | data formatting | bytes 393216
Async XLA Ops:
  1.5 0.7 %copy-start.1 = (f32[8,3,3,3]{0,3,2,1:T(4,128)S(1)}, f32[8,3,3,3]{0,3,2,1:T(4,128)}, u32[]{:S(2)}) copy-start(f32[8,3,3,3]{0,3,2,1:T(4,128)} %param.9) | copy-start | bytes 2596
  52.2 1.7 %copy-start = (f32[8,3,8,256]{3,2,1,0:T(8,128)S(1)}, f32[8,3,8,256]{3,2,1,0:T(8,128)}, u32[]{:S(2)}) copy-start(f32[8,3,8,256]{3,2,1,0:T(8,128)} %get-tuple-element.5) | copy-start | bytes 589828

commit v2 on v1

--- a/solution.py
+++ b/solution.py
@@ -20,10 +20,11 @@
 
 def kernel(
     sizes, material, sten, fac, load, start, out_u, out_r,
-    cor, crhs, res, loc, chain, below, above, cbelow, cabove,
+    cor, crhs, res, loc, chain, chainx, hal, chal, below, above, cbelow, cabove,
     row_out, row_in, crow_out, crow_in, col_out, col_in,
-    gather, maps,
+    gather, maps, grow_out, grow_in, gcol_out, gcol_in,
     row_ss, row_rs, col_ss, col_rs, z_ss, z_rs, map_ss, map_rs, zh_ss, zh_rs,
+    gr_ss, gr_rs, gc_ss, gc_rs,
 ):
     nz, ny, nx = sizes
     layers, comps, rows, lanes = load.shape
@@ -39,9 +40,9 @@
     pending = []
 
     def block(table, level, layer, which):
-        base = material[layer * (2 if level else 1)] * 27 + which * 9
+        mat_id = material[layer * (2 if level else 1)]
         scale = 0.25 if level and table is sten and which == 2 else None
-        values = [[table[base + i * 3 + j] for j in three] for i in three]
+        values = [[table[which, i, j, mat_id] for j in three] for i in three]
         if scale is not None:
             values = [[scale * v for v in line] for line in values]
         return values
@@ -80,6 +81,11 @@
     peers = [(gz != j, at(j, gy, gx)) for j in range(nz)]
     peers += [(has_prev_y, at(gz, gy - 1, gx)), (has_next_y, at(gz, gy + 1, gx))]
     peers += [(has_prev_x, at(gz, gy, gx - 1)), (has_next_x, at(gz, gy, gx + 1))]
+    sides_y = ((has_next_y, gy + 1), (has_prev_y, gy - 1))
+    sides_x = ((has_next_x, gx + 1), (has_prev_x, gx - 1))
+    for j in range(nz):
+        peers += [(jnp.logical_and(gz != j, cond), at(j, spot, gx)) for cond, spot in sides_y]
+        peers += [(jnp.logical_and(gz != j, cond), at(j, gy, spot)) for cond, spot in sides_x]
     for cond, target in peers:
         @pl.when(cond)
         def _(target=target):
@@ -90,10 +96,12 @@
         def _(side=side):
             row_in[:, side] = jnp.zeros_like(row_in[:, side])
             crow_in[:, side] = jnp.zeros_like(crow_in[:, side])
+            grow_in[:, :, side] = jnp.zeros_like(grow_in[:, :, side])
     for side, cond in enumerate((has_prev_x, has_next_x)):
         @pl.when(jnp.logical_not(cond))
         def _(side=side):
             col_in[:, side] = jnp.zeros_like(col_in[:, side])
+            gcol_in[:, :, side] = jnp.zeros_like(gcol_in[:, :, side])
     for cond, ref in ((has_below, below), (has_above, above)):
         @pl.when(jnp.logical_not(cond))
         def _(ref=ref):
@@ -103,6 +111,11 @@
         def _(j=j):
             gather[:, 1, j] = jnp.zeros_like(gather[:, 1, j])
 
+    row_out[:, :, layers * comps :] = jnp.zeros_like(row_out[:, :, layers * comps :])
+    crow_out[:, :, half * comps :] = jnp.zeros_like(crow_out[:, :, half * comps :])
+    grow_out[...] = jnp.zeros_like(grow_out)
+
+    corner_id = lax.broadcasted_iota(jnp.int32, (rows, 128), 1)
     basis_lane = lax.broadcasted_iota(jnp.int32, (8, 128), 1)
     basis = [(basis_lane == c).astype(jnp.float32) for c in three]
     for level, count in ((0, layers), (1, half)):
@@ -124,18 +137,18 @@
             for c in three:
                 maps[gz, level, kind, c] = value[c]
 
-    def held(level, owner, kind):
+    def held(level, owner, kind, width):
         tiles = [maps[owner, level, kind, c] for c in three]
-        return [[jnp.broadcast_to(tiles[i][:rows, j : j + 1], (rows, lanes)) for j in three] for i in three]
-
-    def send_sides(phase, level, field, count):
+        return [[jnp.broadcast_to(tiles[i][:rows, j : j + 1], (rows, width)) for j in three] for i in three]
+
+    def send_sides(phase, level, field, count, tail=None):
         out, into = (crow_out, crow_in) if level else (row_out, row_in)
-        slot = phase - SWEEPS - 1 if level else (phase if phase <= SWEEPS else SWEEPS + 1)
+        slot = phase - SWEEPS - 1 if level else phase
         tiles = [jnp.zeros((rows, wide), jnp.float32)] * 2
-        for layer in range(count):
+        for layer in range(count + (tail is not None)):
             for c in three:
                 spot = layer * comps + c
-                value = field[layer, c]
+                value = field[layer, c] if layer < count else tail[c]
                 out[slot, 0, spot : spot + 1, :] = value[rows - 1 : rows, :]
                 out[slot, 1, spot : spot + 1, :] = value[0:1, :]
                 here = col_id == spot
@@ -181,18 +194,63 @@
             for c in three:
                 res[layer, c] = source[layer, c] - (a[c] - b[c] - d[c])
 
-    def full_residual(level, handle, layer):
-        phase, slot, into = handle
-        edge = []
-        for c in three:
-            spot = layer * comps + c
-            line = jnp.where(top, into[slot, 0, spot : spot + 1, :], 0.0)
-            line = jnp.where(bottom, into[slot, 1, spot : spot + 1, :], line)
-            post = jnp.where(first, col_in[phase, 0][:, spot : spot + 1], 0.0)
-            post = jnp.where(last, col_in[phase, 1][:, spot : spot + 1], post)
-            edge.append(line + post)
+    rim_row = jnp.logical_or(top, bottom)
+    rim_lane = jnp.logical_or(first, last)
+
+    def full_residual(level, layer):
+        rim = chal if level else hal
+        edge = [
+            jnp.where(rim_row, rim[layer, c][:, :lanes], 0.0) + jnp.where(rim_lane, rim[layer, c][:, lanes:], 0.0)
+            for c in three
+        ]
         extra = times(block(sten, level, layer, 1), edge)
         return [res[layer, c] + extra[c] for c in three]
+
+    def rim_tile(prev_row, next_row, prev_col, next_col):
+        return jnp.concatenate(
+            [jnp.where(top, prev_row, next_row), jnp.where(first, prev_col, next_col)], axis=1
+        )
+
+    def sides_tile(handle, spot):
+        phase, slot, into = handle
+        return rim_tile(
+            into[slot, 0, spot : spot + 1, :], into[slot, 1, spot : spot + 1, :],
+            col_in[phase, 0][:, spot : spot + 1], col_in[phase, 1][:, spot : spot + 1],
+        )
+
+    def entry(turn, kind, k, c):
+        rim = rim_tile(
+            grow_in[turn, kind, 0, k, c : c + 1, :], grow_in[turn, kind, 1, k, c : c + 1, :],
+            gcol_in[turn, kind, 0, k][:, c : c + 1], gcol_in[turn, kind, 1, k][:, c : c + 1],
+        )
+        return gather[turn, kind, k, c], rim
+
+    def send_corners(turn, kind, value, wanted):
+        for side, line in ((0, rows - 1), (1, 0)):
+            for c in three:
+                grow_out[turn, kind, side, c : c + 1, :] = value[c][line : line + 1, :]
+        for side, lane in ((0, lanes - 1), (1, 0)):
+            tile = jnp.zeros((rows, 128), jnp.float32)
+            for c in three:
+                tile = jnp.where(corner_id == c, value[c][:, lane : lane + 1], tile)
+            gcol_out[turn, kind, side] = tile
+        for j in range(nz):
+            for side in range(2):
+                cond, spot = sides_y[side]
+                copy_if(jnp.logical_and(wanted(j), cond), grow_out.at[turn, kind, side],
+                        grow_in.at[turn, kind, side, gz],
+                        gr_ss.at[turn, kind, side, j], gr_rs.at[turn, kind, side, gz], at(j, spot, gx))
+                cond, spot = sides_x[side]
+                copy_if(jnp.logical_and(wanted(j), cond), gcol_out.at[turn, kind, side],
+                        gcol_in.at[turn, kind, side, gz],
+                        gc_ss.at[turn, kind, side, j], gc_rs.at[turn, kind, side, gz], at(j, gy, spot))
+
+    def await_corners(turn, kind, j, wanted):
+        for side, (there_y, there_x) in enumerate(((has_prev_y, has_prev_x), (has_next_y, has_next_x))):
+            arrive_if(jnp.logical_and(wanted, there_y), grow_in.at[turn, kind, side, j],
+                      gr_ss.at[turn, kind, side, j], gr_rs.at[turn, kind, side, j])
+            arrive_if(jnp.logical_and(wanted, there_x), gcol_in.at[turn, kind, side, j],
+                      gc_ss.at[turn, kind, side, j], gc_rs.at[turn, kind, side, j])
 
     def line_solve(level, turn, resid, count):
         carry = None
@@ -205,7 +263,9 @@
             carry = now
         for c in three:
             gather[turn, 0, gz, c] = carry[c]
+        ending = carry
         if nz > 1:
+            send_corners(turn, 0, carry, lambda j: jnp.logical_and(gz != j, gz < nz - 1))
             for j in range(nz):
                 copy_if(jnp.logical_and(gz != j, gz < nz - 1), gather.at[turn, 0, gz], gather.at[turn, 0, gz],
                         z_ss.at[turn, 0, j], z_rs.at[turn, 0, gz], at(j, gy, gx))
@@ -219,24 +279,36 @@
             back = now
         for c in three:
             gather[turn, 1, gz, c] = back[c]
+        if nz > 1:
+            send_corners(turn, 1, back, lambda j: gz > j)
         for j in range(nz):
             copy_if(gz > j, gather.at[turn, 1, gz], gather.at[turn, 1, gz],
                     z_ss.at[turn, 1, j], z_rs.at[turn, 1, gz], at(j, gy, gx))
+        handle = send_sides(turn + 1, level, loc, count, ending)
         for j in range(nz - 1):
             arrive_if(gz != j, gather.at[turn, 0, j], z_ss.at[turn, 0, j], z_rs.at[turn, 0, j])
+            await_corners(turn, 0, j, gz != j)
         for j in range(1, nz):
             arrive_if(gz < j, gather.at[turn, 1, j], z_ss.at[turn, 1, j], z_rs.at[turn, 1, j])
-        zero = [jnp.zeros((rows, lanes), jnp.float32)] * 3
+            await_corners(turn, 1, j, gz < j)
+        await_sides(handle)
+        full = 3 * lanes
+        zero = [jnp.zeros((rows, full), jnp.float32)] * 3
         ins, outs = [zero], [zero]
         for k in range(nz - 1):
-            value = [gather[turn, 0, k, c] for c in three]
+            value = []
+            for c in three:
+                own, rim = entry(turn, 0, k, c)
+                rim = jnp.where(gz == k, sides_tile(handle, count * comps + c), rim)
+                value.append(jnp.concatenate([own, rim], axis=1))
             if k:
-                value = [a + b for a, b in zip(value, times(held(level, k, 0), ins[k]))]
+                value = [a + b for a, b in zip(value, times(held(level, k, 0, full), ins[k]))]
             ins.append(value)
         for k in reversed(range(1, nz)):
-            value = [gather[turn, 1, k, c] + b for c, b in enumerate(times(held(level, k, 1), ins[k]))]
+            value = [jnp.concatenate(entry(turn, 1, k, c), axis=1) for c in three]
+            value = [a + b for a, b in zip(value, times(held(level, k, 1, full), ins[k]))]
             if k < nz - 1:
-                value = [a + b for a, b in zip(value, times(held(level, k, 2), outs[0]))]
+                value = [a + b for a, b in zip(value, times(held(level, k, 2, full), outs[0]))]
             outs.insert(0, value)
         enter, leave = ins[0], outs[0]
         for k in range(1, nz):
@@ -246,15 +318,18 @@
         for layer in range(count):
             carry = times(block(fac, level, layer, 1), carry)
             for c in three:
-                chain[layer, c] = carry[c]
+                chainx[layer, c] = carry[c]
+        rim, fresh = (chal, turn == SWEEPS) if level else (hal, False)
         carry = leave
         for layer in reversed(range(count)):
-            carry = [chain[layer, c] + b for c, b in enumerate(times(block(fac, level, layer, 2), carry))]
-            for c in three:
-                loc[layer, c] = loc[layer, c] + carry[c]
-        under = times(held(level, jnp.maximum(gz - 1, 0), 3), [loc[0, c] for c in three])
-        under = [jnp.where(has_below, enter[c] + under[c], 0.0) for c in three]
-        return under, leave
+            carry = [chainx[layer, c] + b for c, b in enumerate(times(block(fac, level, layer, 2), carry))]
+            for c in three:
+                loc[layer, c] = loc[layer, c] + carry[c][:, :lanes]
+                step = sides_tile(handle, layer * comps + c) + carry[c][:, lanes:]
+                rim[layer, c] = step if fresh else rim[layer, c] + step
+        under = times(held(level, jnp.maximum(gz - 1, 0), 3, lanes), [loc[0, c] for c in three])
+        under = [jnp.where(has_below, enter[c][:, :lanes] + under[c], 0.0) for c in three]
+        return under, [leave[c][:, :lanes] for c in three]
 
     pl.semaphore_wait(barrier, total([cond.astype(jnp.int32) for cond, _ in peers]))
 
@@ -268,30 +343,31 @@
     for sweep in range(SWEEPS + 1):
         field = out_u if sweep else start
         inner_residual(0, field, load, below, above, layers)
-        await_sides(handle)
         if sweep == SWEEPS:
             break
         if sweep == 0:
+            await_sides(handle)
+            for layer in range(layers):
+                for c in three:
+                    hal[layer, c] = sides_tile(handle, layer * comps + c)
             for j in range(nz):
                 arrive_if(gz != j, maps.at[j], map_ss.at[j], map_rs.at[j])
-        under, over = line_solve(0, sweep, functools.partial(full_residual, 0, handle), layers)
+        under, over = line_solve(0, sweep, functools.partial(full_residual, 0), layers)
         for layer in range(layers):
             for c in three:
                 out_u[layer, c] = field[layer, c] + loc[layer, c]
         for c in three:
             below[c] = below[c] + under[c]
             above[c] = above[c] + over[c]
-        handle = send_sides(sweep + 1, 0, out_u, layers)
 
     for k in range(half):
-        pair = [full_residual(0, handle, 2 * k + step) for step in range(2)]
+        pair = [full_residual(0, 2 * k + step) for step in range(2)]
         for c in three:
             crhs[k, c] = pair[0][c] + pair[1][c]
     for sweep in range(SWEEPS):
         if sweep:
             inner_residual(1, cor, crhs, cbelow, cabove, half)
-            await_sides(handle)
-            source = functools.partial(full_residual, 1, handle)
+            source = functools.partial(full_residual, 1)
         else:
             def source(layer):
                 return [crhs[layer, c] for c in three]
@@ -303,19 +379,16 @@
         for c in three:
             cbelow[c] = cbelow[c] + under[c] if sweep else under[c]
             cabove[c] = cabove[c] + over[c] if sweep else over[c]
-        if sweep < SWEEPS - 1:
-            handle = send_sides(SWEEPS + 1 + sweep, 1, cor, half)
     for layer in range(layers):
         for c in three:
             out_u[layer, c] = out_u[layer, c] + cor[layer // 2, c]
+            hal[layer, c] = hal[layer, c] + chal[layer // 2, c]
     for c in three:
         below[c] = below[c] + cbelow[c]
         above[c] = above[c] + cabove[c]
-    handle = send_sides(2 * SWEEPS, 0, out_u, layers)
     inner_residual(0, out_u, load, below, above, layers)
-    await_sides(handle)
     for layer in range(layers):
-        value = full_residual(0, handle, layer)
+        value = full_residual(0, layer)
         for c in three:
             out_r[layer, c] = value[c]
     for cond, copy in pending:
@@ -331,7 +404,8 @@
     def on_device(right_side, start_field, layer_material, stiffness, line_factors):
         layers, comps, rows, lanes = right_side.shape
         half = layers // 2
-        wide = -(-layers * comps // 128) * 128
+        wide = -(-(layers + 1) * comps // 128) * 128
+        tall, ctall = (-(-(n + 1) * comps // 8) * 8 for n in (layers, half))
         phases = 2 * SWEEPS + 1
         f32 = jnp.float32
         vmem = pl.BlockSpec(memory_space=pltpu.VMEM)
@@ -343,17 +417,25 @@
             pltpu.VMEM((layers, comps, rows, lanes), f32),
             pltpu.VMEM((layers, comps, rows, lanes), f32),
             pltpu.VMEM((layers, comps, rows, lanes), f32),
+            pltpu.VMEM((layers, comps, rows, 3 * lanes), f32),
+            pltpu.VMEM((layers, comps, rows, 2 * lanes), f32),
+            pltpu.VMEM((half, comps, rows, 2 * lanes), f32),
         ]
         scratch += [pltpu.VMEM((comps, rows, lanes), f32)] * 4
-        scratch += [pltpu.VMEM((SWEEPS + 2, 2, layers * comps, lanes), f32)] * 2
-        scratch += [pltpu.VMEM((SWEEPS - 1, 2, half * comps, lanes), f32)] * 2
+        scratch += [pltpu.VMEM((SWEEPS + 1, 2, tall, lanes), f32)] * 2
+        scratch += [pltpu.VMEM((SWEEPS, 2, ctall, lanes), f32)] * 2
         scratch += [pltpu.VMEM((phases, 2, rows, wide), f32)] * 2
         scratch += [
             pltpu.VMEM((2 * SWEEPS, 2, nz, comps, rows, lanes), f32),
             pltpu.VMEM((nz, 2, 4, comps, 8, 128), f32),
+            pltpu.VMEM((2 * SWEEPS, 2, 2, 8, lanes), f32),
+            pltpu.VMEM((2 * SWEEPS, 2, 2, nz, 8, lanes), f32),
+            pltpu.VMEM((2 * SWEEPS, 2, 2, rows, 128), f32),
+            pltpu.VMEM((2 * SWEEPS, 2, 2, nz, rows, 128), f32),
         ]
         scratch += [dma((phases, 2))] * 4 + [dma((2 * SWEEPS, 2, nz))] * 2
         scratch += [dma((nz,))] * 2 + [dma((2,))] * 2
+        scratch += [dma((2 * SWEEPS, 2, 2, nz))] * 4
         out = jax.ShapeDtypeStruct(right_side.shape, f32)
         return pl.pallas_call(
             functools.partial(kernel, sizes),
@@ -362,7 +444,7 @@
             out_specs=(vmem, vmem),
             scratch_shapes=scratch,
             compiler_params=pltpu.CompilerParams(collective_id=0, has_side_effects=True),
-        )(layer_material, stiffness.reshape(-1), line_factors.reshape(-1), right_side, start_field)
+        )(layer_material, stiffness.transpose(1, 2, 3, 0), line_factors.transpose(1, 2, 3, 0), right_side, start_field)
 
     return jax.shard_map(
         on_device,

time: 54.8 us -> 41.7 us (0.76)
  Pallas kernels: 49.2 us -> 38.5 us
  local copies, waits for them, and re-layouts: 4.76 us -> 2.34 us
    pallas_call x1, Pallas kernels: 49.2 us -> 38.5 us  [on_device(): pl.pallas_call(functools.partial(kernel, sizes), out_shape=(out, out), in...]
    reshape x2 -> x0, local copies, waits for them, and re-layouts: 1.44 us -> none  [the longest x1 0.72 us: on_device(): line_factors.reshape(-1)]
    unnamed x8 -> x4, local copies, waits for them, and re-layouts: 3.33 us -> 2.34 us
where the time goes in v2:
time: 41.7 us; the launch traced here: 41.5 us
  Pallas kernels  38.5 us (92%)
  local copies, waits for them, and re-layouts  2.34 us (6%)
  between operations  0.65 us (2%)
    pallas_call x1, Pallas kernels, on_device(): pl.pallas_call(functools.partial(kernel, sizes), out_shape=(out, out), in...  38.5 us
    unnamed x4, local copies, waits for them, and re-layouts  2.34 us

profile of v2, /device:TPU:0, one launch (start us, length us, event | category | flops | bytes accessed | tf_op | source)
XLA Modules:
  0.0 41.5 jit_solution(17405745817516642027)
XLA Ops:
  0.6 38.5 %shard_map.68 = (f32[8,3,8,256]{3,2,1,0:T(8,128)}, f32[8,3,8,256]{3,2,1,0:T(8,128)}) custom-call(s32[8]{0:T(128)} %material.1, f32[3,3,3,8]{3,2,1,0:T(4,128)} %bitcast.2, f32[3,3,3,8]{3,2,1,0:T(4,128)} %bitcast.3, f32[8,3,8,256]{3,2,1,0:T(8,128)} %load.1, f32[8,3,8,256]{3,2,1,0:T(8,128)} %start.1), custom_call_target="tpu_custom_call" | custom-call | tf_op jit(solution)/shard_map/pallas_call | solution.py:440
  39.2 0.0 copy-start
  39.2 1.7 %copy.9 = f32[8,3,8,256]{3,2,1,0:T(8,128)} copy(f32[8,3,8,256]{3,2,1,0:T(8,128)} %get-tuple-element.4) | data formatting | bytes 393216
  40.8 0.0 copy-done
  40.8 0.7 %copy.10 = f32[8,3,8,256]{3,2,1,0:T(8,128)} copy(f32[8,3,8,256]{3,2,1,0:T(8,128)S(1)} %copy-done) | data formatting | bytes 393216
Async XLA Ops:
  39.2 1.7 %copy-start = (f32[8,3,8,256]{3,2,1,0:T(8,128)S(1)}, f32[8,3,8,256]{3,2,1,0:T(8,128)}, u32[]{:S(2)}) copy-start(f32[8,3,8,256]{3,2,1,0:T(8,128)} %get-tuple-element.5) | copy-start | bytes 589828

commit v3 on v2

--- a/solution.py
+++ b/solution.py
@@ -285,13 +285,18 @@
             copy_if(gz > j, gather.at[turn, 1, gz], gather.at[turn, 1, gz],
                     z_ss.at[turn, 1, j], z_rs.at[turn, 1, gz], at(j, gy, gx))
         handle = send_sides(turn + 1, level, loc, count, ending)
+        await_sides(handle)
+        halo, fresh = (chal, turn == SWEEPS) if level else (hal, False)
+        for layer in range(count):
+            for c in three:
+                step = sides_tile(handle, layer * comps + c)
+                halo[layer, c] = step if fresh else halo[layer, c] + step
         for j in range(nz - 1):
             arrive_if(gz != j, gather.at[turn, 0, j], z_ss.at[turn, 0, j], z_rs.at[turn, 0, j])
             await_corners(turn, 0, j, gz != j)
         for j in range(1, nz):
             arrive_if(gz < j, gather.at[turn, 1, j], z_ss.at[turn, 1, j], z_rs.at[turn, 1, j])
             await_corners(turn, 1, j, gz < j)
-        await_sides(handle)
         full = 3 * lanes
         zero = [jnp.zeros((rows, full), jnp.float32)] * 3
         ins, outs = [zero], [zero]
@@ -319,14 +324,12 @@
             carry = times(block(fac, level, layer, 1), carry)
             for c in three:
                 chainx[layer, c] = carry[c]
-        rim, fresh = (chal, turn == SWEEPS) if level else (hal, False)
         carry = leave
         for layer in reversed(range(count)):
             carry = [chainx[layer, c] + b for c, b in enumerate(times(block(fac, level, layer, 2), carry))]
             for c in three:
                 loc[layer, c] = loc[layer, c] + carry[c][:, :lanes]
-                step = sides_tile(handle, layer * comps + c) + carry[c][:, lanes:]
-                rim[layer, c] = step if fresh else rim[layer, c] + step
+                halo[layer, c] = halo[layer, c] + carry[c][:, lanes:]
         under = times(held(level, jnp.maximum(gz - 1, 0), 3, lanes), [loc[0, c] for c in three])
         under = [jnp.where(has_below, enter[c][:, :lanes] + under[c], 0.0) for c in three]
         return under, [leave[c][:, :lanes] for c in three]

time: 41.7 us -> 42.3 us (1.014)
  Pallas kernels: 38.5 us -> 39.1 us
    pallas_call x1, Pallas kernels: 38.5 us -> 39.1 us  [on_device(): pl.pallas_call(functools.partial(kernel, sizes), out_shape=(out, out), in...]
where the time goes in v3:
time: 42.3 us; the launch traced here: 42.1 us
  Pallas kernels  39.1 us (92%)
  local copies, waits for them, and re-layouts  2.34 us (6%)
  between operations  0.65 us (2%)
    pallas_call x1, Pallas kernels, on_device(): pl.pallas_call(functools.partial(kernel, sizes), out_shape=(out, out), in...  39.1 us
    unnamed x4, local copies, waits for them, and re-layouts  2.34 us

profile of v3, /device:TPU:0, one launch (start us, length us, event | category | flops | bytes accessed | tf_op | source)
XLA Modules:
  0.0 42.1 jit_solution(17926801805535118833)
XLA Ops:
  0.6 39.1 %shard_map.68 = (f32[8,3,8,256]{3,2,1,0:T(8,128)}, f32[8,3,8,256]{3,2,1,0:T(8,128)}) custom-call(s32[8]{0:T(128)} %material.1, f32[3,3,3,8]{3,2,1,0:T(4,128)} %bitcast.2, f32[3,3,3,8]{3,2,1,0:T(4,128)} %bitcast.3, f32[8,3,8,256]{3,2,1,0:T(8,128)} %load.1, f32[8,3,8,256]{3,2,1,0:T(8,128)} %start.1), custom_call_target="tpu_custom_call" | custom-call | tf_op jit(solution)/shard_map/pallas_call | solution.py:443
  39.8 0.0 copy-start
  39.8 1.7 %copy.9 = f32[8,3,8,256]{3,2,1,0:T(8,128)} copy(f32[8,3,8,256]{3,2,1,0:T(8,128)} %get-tuple-element.4) | data formatting | bytes 393216
  41.4 0.0 copy-done
  41.4 0.7 %copy.10 = f32[8,3,8,256]{3,2,1,0:T(8,128)} copy(f32[8,3,8,256]{3,2,1,0:T(8,128)S(1)} %copy-done) | data formatting | bytes 393216
Async XLA Ops:
  39.8 1.7 %copy-start = (f32[8,3,8,256]{3,2,1,0:T(8,128)S(1)}, f32[8,3,8,256]{3,2,1,0:T(8,128)}, u32[]{:S(2)}) copy-start(f32[8,3,8,256]{3,2,1,0:T(8,128)} %get-tuple-element.5) | copy-start | bytes 589828
